TPU v7x, 256 devices: a 8x8x2 block of a 8x8x16 slice. The times are simulated.
256 devices in a mesh: img: 2 (over z), ga: 16 (over y, core), band: 8 (over x).
Axes of the slice: x: 8, y: 8, z: 2, core: 2. Of those that a mesh axis runs over, the one named last changes fastest.
The devices are a block of a 8x8x16 slice.
Arguments:
- orbitals: bfloat16 [1536, 49152], P(('img', 'band'), 'ga'), parts along dimension 0, as said below
- kernel: float32 [49152], P('ga'), may hold values from 0.3 to 3
- block_vectors: bfloat16 [512, 49152], P(('img', 'band'), 'ga'), parts along dimension 0
Outputs:
- ace_vectors: bfloat16 [1536, 49152], P(('img', 'band'), 'ga'), parts along dimension 0
- exchange_block: bfloat16 [512, 49152], P(('img', 'band'), 'ga'), parts along dimension 0
There are 2 independent parts, one for each index of `img`. A program takes and returns all parts, laid end to end along the dimension named above; an argument that names none is the same for every part. Nothing has to cross between parts.
Inputs may be any that keep to these rules, and one draw needn't show every extreme that they name: `orbitals`: the bands of one image are linearly independent, and the block lies largely in their span.
All inputs are finite; a program needn't handle non-finite values.
Results may differ from a plain program's by a relative error of at most 0.02.
Values may be sent and summed in bfloat16 or wider, within the bound.
A program may use at most 64 MiB of HBM per device.

v0:
```python
import jax
import jax.numpy as jnp
from jax import lax
from jax.sharding import PartitionSpec as P


def over_pieces(shard, axis):
    pieces = lax.all_gather(shard, axis).astype(jnp.float32)
    return pieces.sum(axis=0)


def from_everyone(shard, axis):
    count = lax.axis_size(axis)
    return lax.all_to_all(
        jnp.broadcast_to(shard[None], (count, *shard.shape)), axis, 0, 0, tiled=True
    )


def in_order(pieces, dim):
    pieces = jnp.moveaxis(pieces, 0, dim)
    dims = pieces.shape
    return pieces.reshape(*dims[:dim], dims[dim] * dims[dim + 1], *dims[dim + 2 :])


def gathered_copies(shard, axis, dim):
    pieces = from_everyone(shard, axis)
    return in_order(pieces, dim)


def taken_together(shard, axis):
    return from_everyone(shard, axis).astype(jnp.float32).sum(axis=0)


def cut_along(shard, dim, count):
    dims = shard.shape
    pieces = shard.reshape(*dims[:dim], count, dims[dim] // count, *dims[dim + 1 :])
    return jnp.moveaxis(pieces, dim, 0)


def sent_and_summed(shard, axis, dim):
    pieces = cut_along(shard, dim, lax.axis_size(axis))
    arrived = lax.all_to_all(pieces, axis, split_axis=0, concat_axis=0, tiled=True)
    return arrived.astype(jnp.float32).sum(axis=0)


def contract_first(left, right):
    return lax.dot_general(left, right, (((0,), (0,)), ((), ())), precision=lax.Precision.HIGHEST)


def shards(orbitals, kernel, block_vectors):
    groups = lax.axis_size("ga")
    own_band = lax.axis_index("band")
    total_coeffs = orbitals.shape[1] * groups
    full_orbitals, full_block = (
        lax.all_gather(orbitals, "band", axis=0, tiled=True),
        lax.all_gather(block_vectors, "band", axis=0, tiled=True),
    )
    weighted = (-(full_orbitals.astype(jnp.float32) * kernel[None, :])).astype(jnp.bfloat16)
    own_rows = orbitals.shape[0]
    partial_rows = lax.dot_general(
        orbitals, weighted, (((1,), (1,)), ((), ())), preferred_element_type=jnp.float32
    )
    summed_rows = over_pieces(partial_rows.astype(jnp.bfloat16), "ga").astype(jnp.float32)
    margin = (
        -gathered_copies(summed_rows.astype(jnp.bfloat16), "band", 0).astype(summed_rows.dtype)
        / total_coeffs
    )
    factor = jnp.linalg.cholesky(margin)
    identity = jnp.eye(factor.shape[0], dtype=jnp.float32)
    inverse = lax.linalg.triangular_solve(factor, identity, left_side=True, lower=True)
    inverse_rows = lax.dynamic_slice_in_dim(inverse, own_band * own_rows, own_rows, 0)
    projector = jnp.dot(inverse_rows, weighted.astype(jnp.float32), precision=lax.Precision.HIGHEST)
    local_coupling = jnp.dot(
        projector, full_block.astype(jnp.float32).T, precision=lax.Precision.HIGHEST
    )
    coupling = (
        taken_together(local_coupling.astype(jnp.bfloat16), "ga").astype(jnp.float32) / total_coeffs
    )
    applied = sent_and_summed(
        (-contract_first(coupling, projector)).astype(jnp.bfloat16), "band", 0
    )
    return (projector.astype(jnp.bfloat16), applied.astype(jnp.bfloat16))


def solution(mesh):
    placed = (P(("img", "band"), "ga"), P("ga"), P(("img", "band"), "ga"))
    return jax.shard_map(
        shards,
        mesh=mesh,
        in_specs=placed,
        out_specs=(P(("img", "band"), "ga"), P(("img", "band"), "ga")),
        check_vma=False,
    )
```

profile of v0, /device:TPU:513, one launch (start us, length us, event | category | flops | bytes accessed | tf_op | source)
XLA Modules:
  0.0 510.3 jit_solution(14080767505893318742)
XLA Ops:
  8.0 80.9 %all-gather.5.cloned.1.call-done = bf16[768,3072]{1,0:T(8,128)(2,1)} async-done(((bf16[96,3072]{1,0:T(8,128)(2,1)}), bf16[768,3072]{1,0:T(8,128)(2,1)}) %all-gather.5.cloned.1.call-update) | async-done | bytes 4718608 | tf_op jit(solution)/shard_map/all_gather | solution.py:55
  89.0 4.8 fusion.21
  93.8 41.2 %all-gather.9.cloned.1.call-done = bf16[1536,768]{1,0:T(8,128)(2,1)} async-done(((bf16[96,768]{1,0:T(8,128)(2,1)}), bf16[1536,768]{1,0:T(8,128)(2,1)}) %all-gather.9.cloned.1.call-update) | async-done | bytes 2359312 | tf_op jit(solution)/shard_map/all_gather | solution.py:8
  138.0 6.4 %all-to-all-start = ((bf16[8,96,768]{2,1,0:T(8,128)(2,1)}), bf16[8,96,768]{2,1,0:T(8,128)(2,1)S(1)}, u32[]{:S(2)}, u32[]{:S(2)}) async-start(bf16[8,96,768]{2,1,0:T(8,128)(2,1)} %broadcast_in_dim.5), calls=%async_computation | async-start | bytes 2359296 | tf_op jit(solution)/shard_map/all_to_all | solution.py:14
  147.9 35.2 %all-to-all-done = bf16[8,96,768]{2,1,0:T(8,128)(2,1)S(1)} async-done(((bf16[8,96,768]{2,1,0:T(8,128)(2,1)}), bf16[8,96,768]{2,1,0:T(8,128)(2,1)S(1)}, u32[]{:S(2)}, u32[]{:S(2)}) %all-to-all-start) | async-done | bytes 1179680 | tf_op jit(solution)/shard_map/all_to_all | solution.py:14
  183.3 2.2 copy.7
  188.9 11.7 %cholesky.165 = f32[128,128]{1,0:T(8,128)S(1)} custom-call(f32[128,128]{1,0:T(8,128)S(1)} %cholesky.424), custom_call_target="Cholesky" | custom-call | tf_op jit(solution)/shard_map/jit(cholesky)/cholesky | solution.py:68
  200.6 9.8 %custom-call.46 = f32[1,128,128]{1,2,0:T(8,128)S(1)} custom-call(f32[1,128,128]{2,1,0:T(8,128)S(1)} %get-tuple-element.45), custom_call_target="InvertDiagBlocksLowerTriangular" | custom-call | tf_op jit(solution)/shard_map/jit(cholesky)/cholesky | solution.py:68
  213.4 11.7 %cholesky.188 = f32[128,128]{1,0:T(8,128)S(1)} custom-call(f32[128,128]{1,0:T(8,128)S(1)} %cholesky.428), custom_call_target="Cholesky" | custom-call | tf_op jit(solution)/shard_map/jit(cholesky)/cholesky | solution.py:68
  225.2 10.0 %custom-call.47 = f32[1,128,128]{1,2,0:T(8,128)S(1)} custom-call(f32[1,128,128]{2,1,0:T(8,128)S(1)} %get-tuple-element.42), custom_call_target="InvertDiagBlocksLowerTriangular" | custom-call | tf_op jit(solution)/shard_map/jit(cholesky)/cholesky | solution.py:68
  237.1 11.7 %cholesky.354 = f32[128,128]{1,0:T(8,128)S(1)} custom-call(f32[128,128]{1,0:T(8,128)S(1)} %cholesky.433), custom_call_target="Cholesky" | custom-call | tf_op jit(solution)/shard_map/jit(cholesky)/cholesky | solution.py:68
  249.5 9.8 %custom-call.48 = f32[1,128,128]{1,2,0:T(8,128)S(1)} custom-call(f32[1,128,128]{2,1,0:T(8,128)S(1)} %get-tuple-element.39), custom_call_target="InvertDiagBlocksLowerTriangular" | custom-call | tf_op jit(solution)/shard_map/jit(cholesky)/cholesky | solution.py:68
  261.2 12.2 %cholesky.373 = f32[128,128]{1,0:T(8,128)S(1)} custom-call(f32[128,128]{1,0:T(8,128)S(1)} %cholesky.438), custom_call_target="Cholesky" | custom-call | tf_op jit(solution)/shard_map/jit(cholesky)/cholesky | solution.py:68
  274.1 9.8 %custom-call.49 = f32[1,128,128]{1,2,0:T(8,128)S(1)} custom-call(f32[1,128,128]{2,1,0:T(8,128)S(1)} %get-tuple-element.36), custom_call_target="InvertDiagBlocksLowerTriangular" | custom-call | tf_op jit(solution)/shard_map/jit(cholesky)/cholesky | solution.py:68
  285.7 11.7 %cholesky.392 = f32[128,128]{1,0:T(8,128)S(1)} custom-call(f32[128,128]{1,0:T(8,128)S(1)} %cholesky.443), custom_call_target="Cholesky" | custom-call | tf_op jit(solution)/shard_map/jit(cholesky)/cholesky | solution.py:68
  298.2 9.8 %custom-call.50 = f32[1,128,128]{1,2,0:T(8,128)S(1)} custom-call(f32[1,128,128]{2,1,0:T(8,128)S(1)} %get-tuple-element.33), custom_call_target="InvertDiagBlocksLowerTriangular" | custom-call | tf_op jit(solution)/shard_map/jit(cholesky)/cholesky | solution.py:68
  309.5 11.9 %cholesky.410 = f32[128,128]{1,0:T(8,128)S(1)} custom-call(f32[128,128]{1,0:T(8,128)S(1)} %convolution_subtract_fusion.8), custom_call_target="Cholesky" | custom-call | tf_op jit(solution)/shard_map/jit(cholesky)/cholesky | solution.py:68
  328.2 21.5 %while.1 = (s32[]{:T(128)}, f32[768,768]{1,0:T(8,128)}, s32[6,2]{0,1:T(2,128)S(1)}, f32[6,128,128]{2,1,0:T(8,128)}, s32[]{:T(128)}) while((s32[]{:T(128)}, f32[768,768]{1,0:T(8,128)}, s32[6,2]{0,1:T(2,128)S(1)}, f32[6,128,128]{2,1,0:T(8,128)}, s32[]{:T(128)}) %tuple.45), condition=%wide.while_cond, body=%wide.while_body.sunk | while | flops 2 | bytes 132705 | solution.py:70
  328.8 2.9 bitcast_dynamic-update-slice_fusion.2
  332.5 2.9 bitcast_dynamic-update-slice_fusion.2
  336.1 2.9 bitcast_dynamic-update-slice_fusion.2
  339.6 2.9 bitcast_dynamic-update-slice_fusion.2
  343.2 2.9 bitcast_dynamic-update-slice_fusion.2
  346.8 2.8 bitcast_dynamic-update-slice_fusion.2
  349.7 59.8 %custom-call.51 = f32[6,128,128]{1,2,0:T(8,128)S(1)} custom-call(f32[6,128,128]{2,1,0:T(8,128)} %get-tuple-element.9), custom_call_target="InvertDiagBlocksLowerTriangular" | custom-call | tf_op jit(solution)/shard_map/triangular_solve | solution.py:70
  417.2 2.0 fusion.12
  419.8 2.3 convolution_subtract_fusion
  422.6 3.7 fusion.65
  426.4 3.0 convolution_convert_fusion
  429.4 27.4 %all_to_all.15 = bf16[16,96,256]{2,1,0:T(8,128)(2,1)S(1)} all-to-all(bf16[16,96,256]{2,1,0:T(8,128)(2,1)S(1)} %broadcast_in_dim.7), channel_id=1, replica_groups=mesh['img'=2,'ga'=16,'band'=8] {'ga'}, dimensions={0} | all-to-all | bytes 1572864 | tf_op jit(solution)/shard_map/all_to_all | solution.py:14
  456.9 2.7 fusion
  459.6 43.0 %all_to_all.16 = bf16[8,32,3072]{2,1,0:T(8,128)(2,1)S(1)} all-to-all(bf16[8,32,3072]{2,1,0:T(8,128)(2,1)S(1)} %bitcast.88), channel_id=1, replica_groups=mesh['img'=2,'ga'=16,'band'=8] {'band'}, dimensions={0} | all-to-all | bytes 3145728 | tf_op jit(solution)/shard_map/all_to_all | solution.py:42
  (79 shorter events, 40.1 us)
Async XLA Ops:
  7.2 81.8 %all-gather.5.cloned.1.call-start = ((), (), s32[]{:S(2)}) async-start(), calls=%async_computation.3 | async-start | bytes 5308416 | tf_op jit(solution)/shard_map/all_gather | solution.py:55
  8.0 127.0 %all-gather.9.cloned.1.call-start = ((), (), s32[]{:S(2)}) async-start(), calls=%async_computation.5 | async-start | bytes 2506752 | tf_op jit(solution)/shard_map/all_gather | solution.py:8
  138.0 45.0 %all-to-all-start = ((bf16[8,96,768]{2,1,0:T(8,128)(2,1)}), bf16[8,96,768]{2,1,0:T(8,128)(2,1)S(1)}, u32[]{:S(2)}, u32[]{:S(2)}) async-start(bf16[8,96,768]{2,1,0:T(8,128)(2,1)} %broadcast_in_dim.5), calls=%async_computation | async-start | bytes 2359296 | tf_op jit(solution)/shard_map/all_to_all | solution.py:14
  144.5 281.9 %all-gather.7.cloned.1.call-start = ((), (), s32[]{:S(2)}) async-start(), calls=%async_computation.4 | async-start | bytes 1769472 | tf_op jit(solution)/shard_map/all_gather | solution.py:56
  187.4 1.5 copy-start.1
  328.2 84.5 %copy-start = (f32[768,768]{1,0:T(8,128)S(1)}, f32[768,768]{1,0:T(8,128)}, u32[]{:S(2)}) copy-start(f32[768,768]{1,0:T(8,128)} %fusion.25) | copy-start | bytes 7077892
  414.7 7.9 %slice-start = ((s8[4718592]{0:T(1024)(128)(4,1)}), s8[4194304]{0:T(1024)(128)(4,1)S(1)}, s32[]{:S(2)}) async-start(s8[4718592]{0:T(1024)(128)(4,1)} %bitcast.90), calls=%async_computation.6 | async-start | bytes 8388608
  417.2 5.4 %slice-start.1 = ((s8[4718592]{0:T(1024)(128)(4,1)}), s8[524288]{0:T(1024)(128)(4,1)S(1)}, s32[]{:S(2)}) async-start(s8[4718592]{0:T(1024)(128)(4,1)} %bitcast.90), calls=%async_computation.7 | async-start | bytes 1048576
  419.2 3.4 copy-start.2
Sparse Core Ops, SparseCore 0:
  9.8 79.1 all-gather.4
  93.9 40.9 all-gather.8
  147.1 44.9 all-gather.6
where the time goes:
time: 514 us; the launch traced here: 510 us
  other arithmetic  193 us (38%)
  waiting for transfers between devices  159 us (31%)
  blocking collectives  70.4 us (14%)
  matrix products  37 us (7%)
  local copies, waits for them, and re-layouts  26.5 us (5%)
  between operations  18.2 us (4%)
  starting transfers between devices  6.6 us (1%)
    another operation x22, other arithmetic, shards(): factor = jnp.linalg.cholesky(margin)  124 us
    all_gather x1, waiting for transfers between devices, shards(): lax.all_gather(orbitals, 'band', axis=0, tiled=True)  80.9 us
    another operation x3, other arithmetic, shards(): lax.linalg.triangular_solve(factor, identity, left_side=True, lower=True)  61.4 us
    all_to_all x1, blocking collectives, sent_and_summed(): lax.all_to_all(pieces, axis, split_axis=0, concat_axis=0, tiled=True)  43 us
    all_gather x1, waiting for transfers between devices, over_pieces(): pieces = lax.all_gather(shard, axis).astype(jnp.float32)  41.2 us
    all_to_all x1, waiting for transfers between devices, from_everyone(): lax.all_to_all(jnp.broadcast_to(shard[None], (count, *shard.shape)), axis...  35.2 us
    all_to_all x1, blocking collectives, from_everyone(): lax.all_to_all(jnp.broadcast_to(shard[None], (count, *shard.shape)), axis...  27.4 us
    another operation x18, local copies, waits for them, and re-layouts  21.5 us
  transfers between devices with their start and end apart: 4, of which 3 were waited for; matrix products, arithmetic and copies ran while one was open for 47% of the time, Pallas kernels for 0%

commit v1 on v0

--- a/solution.py
+++ b/solution.py
@@ -2,6 +2,27 @@
 import jax.numpy as jnp
 from jax import lax
 from jax.sharding import PartitionSpec as P
+
+
+def collect(value, axis, dim):
+    peers, place, rows = (lax.axis_size(axis), lax.axis_index(axis), value.shape[dim])
+    right = [(i, (i + 1) % peers) for i in range(peers)]
+    left = [(i, (i - 1) % peers) for i in range(peers)]
+    result = jnp.zeros((*value.shape[:dim], peers * rows, *value.shape[dim + 1 :]), value.dtype)
+    result = lax.dynamic_update_slice_in_dim(result, value, place * rows, axis=dim)
+    from_left = from_right = value
+    half = peers // 2
+    for lap in range(1, half + 1):
+        from_left = lax.ppermute(from_left, axis, right)
+        result = lax.dynamic_update_slice_in_dim(
+            result, from_left, (place - lap) % peers * rows, axis=dim
+        )
+        if lap < peers - half:
+            from_right = lax.ppermute(from_right, axis, left)
+            result = lax.dynamic_update_slice_in_dim(
+                result, from_right, (place + lap) % peers * rows, axis=dim
+            )
+    return result
 
 
 def over_pieces(shard, axis):
@@ -52,7 +73,7 @@
     own_band = lax.axis_index("band")
     total_coeffs = orbitals.shape[1] * groups
     full_orbitals, full_block = (
-        lax.all_gather(orbitals, "band", axis=0, tiled=True),
+        collect(orbitals, "band", 0),
         lax.all_gather(block_vectors, "band", axis=0, tiled=True),
     )
     weighted = (-(full_orbitals.astype(jnp.float32) * kernel[None, :])).astype(jnp.bfloat16)

time: 514 us -> 518 us (level)
  waiting for transfers between devices: 159 us -> 138 us
  starting transfers between devices: 6.6 us -> 23.9 us
    all_gather x1 -> x0, waiting for transfers between devices: 80.9 us -> none  [shards(): lax.all_gather(orbitals, 'band', axis=0, tiled=True)]
    ppermute x0 -> x7, waiting for transfers between devices: none -> 36.3 us  [the longest x4 36.3 us: collect(): from_left = lax.ppermute(from_left, axis, right)]
    all_gather x1, waiting for transfers between devices: 41.2 us -> 65.9 us  [over_pieces(): pieces = lax.all_gather(shard, axis).astype(jnp.float32)]
    ppermute x0 -> x7, starting transfers between devices: none -> 17.3 us  [the longest x4 9.39 us: collect(): from_left = lax.ppermute(from_left, axis, right)]
  transfers between devices with their start and end apart: 4 -> 10, of which waited for: 3 -> 6; matrix products, arithmetic and copies ran while one was open for 47% -> 47% of each run, Pallas kernels for 0% -> 0%
where the time goes in v1:
time: 518 us; the launch traced here: 510 us
  other arithmetic  193 us (37%)
  waiting for transfers between devices  138 us (27%)
  blocking collectives  70.3 us (14%)
  matrix products  34.5 us (7%)
  local copies, waits for them, and re-layouts  29.6 us (6%)
  starting transfers between devices  23.9 us (5%)
  between operations  20.2 us (4%)
    another operation x22, other arithmetic, shards(): factor = jnp.linalg.cholesky(margin)  124 us
    all_gather x1, waiting for transfers between devices, over_pieces(): pieces = lax.all_gather(shard, axis).astype(jnp.float32)  65.9 us
    another operation x3, other arithmetic, shards(): lax.linalg.triangular_solve(factor, identity, left_side=True, lower=True)  61.4 us
    all_to_all x1, blocking collectives, sent_and_summed(): lax.all_to_all(pieces, axis, split_axis=0, concat_axis=0, tiled=True)  42.9 us
    ppermute x4, waiting for transfers between devices, collect(): from_left = lax.ppermute(from_left, axis, right)  36.3 us
    all_to_all x1, waiting for transfers between devices, from_everyone(): lax.all_to_all(jnp.broadcast_to(shard[None], (count, *shard.shape)), axis...  35.6 us
    all_to_all x1, blocking collectives, from_everyone(): lax.all_to_all(jnp.broadcast_to(shard[None], (count, *shard.shape)), axis...  27.4 us
    another operation x18, local copies, waits for them, and re-layouts  21 us
  transfers between devices with their start and end apart: 10, of which 6 were waited for; matrix products, arithmetic and copies ran while one was open for 47% of the time, Pallas kernels for 0%

profile of v1, /device:TPU:513, one launch (start us, length us, event | category | flops | bytes accessed | tf_op | source)
XLA Modules:
  0.0 509.8 jit_solution(5847782982322109458)
XLA Ops:
  13.9 6.2 %collective-permute-done = bf16[96,3072]{1,0:T(8,128)(2,1)S(1)} collective-permute-done((bf16[96,3072]{1,0:T(8,128)(2,1)}, bf16[96,3072]{1,0:T(8,128)(2,1)S(1)}, u32[]{:S(2)}, u32[]{:S(2)}) %collective-permute-start) | collective-permute-done | bytes 589856 | tf_op jit(solution)/shard_map/ppermute | solution.py:16
  20.1 4.0 collective-permute-start.2
  24.1 2.9 collective-permute-start.3
  27.2 8.9 %collective-permute-done.2 = bf16[96,3072]{1,0:T(8,128)(2,1)S(1)} collective-permute-done((bf16[96,3072]{1,0:T(8,128)(2,1)S(1)}, bf16[96,3072]{1,0:T(8,128)(2,1)S(1)}, u32[]{:S(2)}, u32[]{:S(2)}) %collective-permute-start.2) | collective-permute-done | bytes 589856 | tf_op jit(solution)/shard_map/ppermute | solution.py:16
  38.8 9.0 %collective-permute-done.4 = bf16[96,3072]{1,0:T(8,128)(2,1)S(1)} collective-permute-done((bf16[96,3072]{1,0:T(8,128)(2,1)S(1)}, bf16[96,3072]{1,0:T(8,128)(2,1)S(1)}, u32[]{:S(2)}, u32[]{:S(2)}) %collective-permute-start.4) | collective-permute-done | bytes 589856 | tf_op jit(solution)/shard_map/ppermute | solution.py:16
  47.8 3.1 collective-permute-start.6
  51.0 12.3 %collective-permute-done.6 = bf16[96,3072]{1,0:T(8,128)(2,1)S(1)} collective-permute-done((bf16[96,3072]{1,0:T(8,128)(2,1)S(1)}, bf16[96,3072]{1,0:T(8,128)(2,1)S(1)}, u32[]{:S(2)}, u32[]{:S(2)}) %collective-permute-start.6) | collective-permute-done | bytes 589856 | tf_op jit(solution)/shard_map/ppermute | solution.py:16
  67.8 65.9 %all-gather.6.cloned.1.call-done = bf16[1536,768]{1,0:T(8,128)(2,1)} async-done(((bf16[96,768]{1,0:T(8,128)(2,1)}), bf16[1536,768]{1,0:T(8,128)(2,1)}) %all-gather.6.cloned.1.call-update) | async-done | bytes 2359312 | tf_op jit(solution)/shard_map/all_gather | solution.py:29
  136.8 6.4 %all-to-all-start = ((bf16[8,96,768]{2,1,0:T(8,128)(2,1)}), bf16[8,96,768]{2,1,0:T(8,128)(2,1)S(1)}, u32[]{:S(2)}, u32[]{:S(2)}) async-start(bf16[8,96,768]{2,1,0:T(8,128)(2,1)} %broadcast_in_dim.9), calls=%async_computation | async-start | bytes 2359296 | tf_op jit(solution)/shard_map/all_to_all | solution.py:35
  146.5 35.6 %all-to-all-done = bf16[8,96,768]{2,1,0:T(8,128)(2,1)S(1)} async-done(((bf16[8,96,768]{2,1,0:T(8,128)(2,1)}), bf16[8,96,768]{2,1,0:T(8,128)(2,1)S(1)}, u32[]{:S(2)}, u32[]{:S(2)}) %all-to-all-start) | async-done | bytes 1179680 | tf_op jit(solution)/shard_map/all_to_all | solution.py:35
  187.9 11.7 %cholesky.165 = f32[128,128]{1,0:T(8,128)S(1)} custom-call(f32[128,128]{1,0:T(8,128)S(1)} %cholesky.424), custom_call_target="Cholesky" | custom-call | tf_op jit(solution)/shard_map/jit(cholesky)/cholesky | solution.py:89
  199.8 9.8 %custom-call.46 = f32[1,128,128]{1,2,0:T(8,128)S(1)} custom-call(f32[1,128,128]{2,1,0:T(8,128)S(1)} %get-tuple-element.45), custom_call_target="InvertDiagBlocksLowerTriangular" | custom-call | tf_op jit(solution)/shard_map/jit(cholesky)/cholesky | solution.py:89
  212.5 11.7 %cholesky.188 = f32[128,128]{1,0:T(8,128)S(1)} custom-call(f32[128,128]{1,0:T(8,128)S(1)} %cholesky.428), custom_call_target="Cholesky" | custom-call | tf_op jit(solution)/shard_map/jit(cholesky)/cholesky | solution.py:89
  224.2 10.2 %custom-call.47 = f32[1,128,128]{1,2,0:T(8,128)S(1)} custom-call(f32[1,128,128]{2,1,0:T(8,128)S(1)} %get-tuple-element.42), custom_call_target="InvertDiagBlocksLowerTriangular" | custom-call | tf_op jit(solution)/shard_map/jit(cholesky)/cholesky | solution.py:89
  236.3 11.7 %cholesky.354 = f32[128,128]{1,0:T(8,128)S(1)} custom-call(f32[128,128]{1,0:T(8,128)S(1)} %cholesky.433), custom_call_target="Cholesky" | custom-call | tf_op jit(solution)/shard_map/jit(cholesky)/cholesky | solution.py:89
  248.7 9.8 %custom-call.48 = f32[1,128,128]{1,2,0:T(8,128)S(1)} custom-call(f32[1,128,128]{2,1,0:T(8,128)S(1)} %get-tuple-element.39), custom_call_target="InvertDiagBlocksLowerTriangular" | custom-call | tf_op jit(solution)/shard_map/jit(cholesky)/cholesky | solution.py:89
  260.4 11.9 %cholesky.373 = f32[128,128]{1,0:T(8,128)S(1)} custom-call(f32[128,128]{1,0:T(8,128)S(1)} %cholesky.438), custom_call_target="Cholesky" | custom-call | tf_op jit(solution)/shard_map/jit(cholesky)/cholesky | solution.py:89
  273.1 9.8 %custom-call.49 = f32[1,128,128]{1,2,0:T(8,128)S(1)} custom-call(f32[1,128,128]{2,1,0:T(8,128)S(1)} %get-tuple-element.36), custom_call_target="InvertDiagBlocksLowerTriangular" | custom-call | tf_op jit(solution)/shard_map/jit(cholesky)/cholesky | solution.py:89
  284.6 11.7 %cholesky.392 = f32[128,128]{1,0:T(8,128)S(1)} custom-call(f32[128,128]{1,0:T(8,128)S(1)} %cholesky.443), custom_call_target="Cholesky" | custom-call | tf_op jit(solution)/shard_map/jit(cholesky)/cholesky | solution.py:89
  297.1 9.8 %custom-call.50 = f32[1,128,128]{1,2,0:T(8,128)S(1)} custom-call(f32[1,128,128]{2,1,0:T(8,128)S(1)} %get-tuple-element.33), custom_call_target="InvertDiagBlocksLowerTriangular" | custom-call | tf_op jit(solution)/shard_map/jit(cholesky)/cholesky | solution.py:89
  308.4 11.9 %cholesky.410 = f32[128,128]{1,0:T(8,128)S(1)} custom-call(f32[128,128]{1,0:T(8,128)S(1)} %convolution_subtract_fusion.8), custom_call_target="Cholesky" | custom-call | tf_op jit(solution)/shard_map/jit(cholesky)/cholesky | solution.py:89
  327.1 21.0 %while.1 = (s32[]{:T(128)}, f32[768,768]{1,0:T(8,128)}, s32[6,2]{0,1:T(2,128)S(1)}, f32[6,128,128]{2,1,0:T(8,128)}, s32[]{:T(128)}) while((s32[]{:T(128)}, f32[768,768]{1,0:T(8,128)}, s32[6,2]{0,1:T(2,128)S(1)}, f32[6,128,128]{2,1,0:T(8,128)}, s32[]{:T(128)}) %tuple.45), condition=%wide.while_cond, body=%wide.while_body.sunk | while | flops 2 | bytes 132705 | solution.py:91
  327.8 3.0 bitcast_dynamic-update-slice_fusion.2
  331.3 2.9 bitcast_dynamic-update-slice_fusion.2
  334.9 2.9 bitcast_dynamic-update-slice_fusion.2
  338.3 2.9 bitcast_dynamic-update-slice_fusion.2
  341.8 2.9 bitcast_dynamic-update-slice_fusion.2
  348.1 59.8 %custom-call.51 = f32[6,128,128]{1,2,0:T(8,128)S(1)} custom-call(f32[6,128,128]{2,1,0:T(8,128)} %get-tuple-element.9), custom_call_target="InvertDiagBlocksLowerTriangular" | custom-call | tf_op jit(solution)/shard_map/triangular_solve | solution.py:91
  421.1 3.7 fusion.65
  424.9 3.0 convolution_convert_fusion
  427.9 27.4 %all_to_all.15 = bf16[16,96,256]{2,1,0:T(8,128)(2,1)S(1)} all-to-all(bf16[16,96,256]{2,1,0:T(8,128)(2,1)S(1)} %broadcast_in_dim.10), channel_id=1, replica_groups=mesh['img'=2,'ga'=16,'band'=8] {'ga'}, dimensions={0} | all-to-all | bytes 1572864 | tf_op jit(solution)/shard_map/all_to_all | solution.py:35
  458.1 42.9 %all_to_all.16 = bf16[8,32,3072]{2,1,0:T(8,128)(2,1)S(1)} all-to-all(bf16[8,32,3072]{2,1,0:T(8,128)(2,1)S(1)} %bitcast.88), channel_id=1, replica_groups=mesh['img'=2,'ga'=16,'band'=8] {'band'}, dimensions={0} | all-to-all | bytes 3145728 | tf_op jit(solution)/shard_map/all_to_all | solution.py:63
  (103 shorter events, 64.0 us)
Async XLA Ops:
  8.0 125.7 %all-gather.6.cloned.1.call-start = ((), (), s32[]{:S(2)}) async-start(), calls=%async_computation.4 | async-start | bytes 2506752 | tf_op jit(solution)/shard_map/all_gather | solution.py:29
  8.1 12.0 %collective-permute-start = (bf16[96,3072]{1,0:T(8,128)(2,1)}, bf16[96,3072]{1,0:T(8,128)(2,1)S(1)}, u32[]{:S(2)}, u32[]{:S(2)}) collective-permute-start(bf16[96,3072]{1,0:T(8,128)(2,1)} %param.3), channel_id=1, source_target_pairs={{0,1},{1,2},{2,3},{3,4},{4,5},{5,6},{6,7},{7,0},{8,9},{9,10},{10,1... | collective-permute-start | bytes 1769480 | tf_op jit(solution)/shard_map/ppermute | solution.py:16
  10.4 13.7 %collective-permute-start.1 = (bf16[96,3072]{1,0:T(8,128)(2,1)}, bf16[96,3072]{1,0:T(8,128)(2,1)S(1)}, u32[]{:S(2)}, u32[]{:S(2)}) collective-permute-start(bf16[96,3072]{1,0:T(8,128)(2,1)} %param.3), channel_id=1, source_target_pairs={{0,7},{1,0},{2,1},{3,2},{4,3},{5,4},{6,5},{7,6},{8,15},{9,8},{10,9... | collective-permute-start | bytes 1769480 | tf_op jit(solution)/shard_map/ppermute | solution.py:21
  12.7 1.1 copy-start.3
  20.1 16.0 %collective-permute-start.2 = (bf16[96,3072]{1,0:T(8,128)(2,1)S(1)}, bf16[96,3072]{1,0:T(8,128)(2,1)S(1)}, u32[]{:S(2)}, u32[]{:S(2)}) collective-permute-start(bf16[96,3072]{1,0:T(8,128)(2,1)S(1)} %collective-permute-done), channel_id=1, source_target_pairs={{0,1},{1,2},{2,3},{3,4},{4,5},{5,6},{6,7},{7,0},{8,9},{9,10},{10,1... | collective-permute-start | bytes 1769480 | tf_op jit(solution)/shard_map/ppermute | solution.py:16
  24.1 11.9 %collective-permute-start.3 = (bf16[96,3072]{1,0:T(8,128)(2,1)S(1)}, bf16[96,3072]{1,0:T(8,128)(2,1)S(1)}, u32[]{:S(2)}, u32[]{:S(2)}) collective-permute-start(bf16[96,3072]{1,0:T(8,128)(2,1)S(1)} %collective-permute-done.1), channel_id=1, source_target_pairs={{0,7},{1,0},{2,1},{3,2},{4,3},{5,4},{6,5},{7,6},{8,15},{9,8},{10,9... | collective-permute-start | bytes 1769480 | tf_op jit(solution)/shard_map/ppermute | solution.py:21
  36.0 11.8 %collective-permute-start.4 = (bf16[96,3072]{1,0:T(8,128)(2,1)S(1)}, bf16[96,3072]{1,0:T(8,128)(2,1)S(1)}, u32[]{:S(2)}, u32[]{:S(2)}) collective-permute-start(bf16[96,3072]{1,0:T(8,128)(2,1)S(1)} %collective-permute-done.2), channel_id=1, source_target_pairs={{0,1},{1,2},{2,3},{3,4},{4,5},{5,6},{6,7},{7,0},{8,9},{9,10},{10,1... | collective-permute-start | bytes 1769480 | tf_op jit(solution)/shard_map/ppermute | solution.py:16
  36.0 14.9 %collective-permute-start.5 = (bf16[96,3072]{1,0:T(8,128)(2,1)S(1)}, bf16[96,3072]{1,0:T(8,128)(2,1)S(1)}, u32[]{:S(2)}, u32[]{:S(2)}) collective-permute-start(bf16[96,3072]{1,0:T(8,128)(2,1)S(1)} %collective-permute-done.3), channel_id=1, source_target_pairs={{0,7},{1,0},{2,1},{3,2},{4,3},{5,4},{6,5},{7,6},{8,15},{9,8},{10,9... | collective-permute-start | bytes 1769480 | tf_op jit(solution)/shard_map/ppermute | solution.py:21
  38.8 26.7 %copy-start.4 = (f32[3072]{0:T(1024)S(1)}, f32[3072]{0:T(1024)}, u32[]{:S(2)}) copy-start(f32[3072]{0:T(1024)} %param.4) | copy-start | bytes 36868
  47.8 15.5 %collective-permute-start.6 = (bf16[96,3072]{1,0:T(8,128)(2,1)S(1)}, bf16[96,3072]{1,0:T(8,128)(2,1)S(1)}, u32[]{:S(2)}, u32[]{:S(2)}) collective-permute-start(bf16[96,3072]{1,0:T(8,128)(2,1)S(1)} %collective-permute-done.4), channel_id=1, source_target_pairs={{0,1},{1,2},{2,3},{3,4},{4,5},{5,6},{6,7},{7,0},{8,9},{9,10},{10,1... | collective-permute-start | bytes 1769480 | tf_op jit(solution)/shard_map/ppermute | solution.py:16
  63.4 2.1 copy-start.2
  136.8 45.2 %all-to-all-start = ((bf16[8,96,768]{2,1,0:T(8,128)(2,1)}), bf16[8,96,768]{2,1,0:T(8,128)(2,1)S(1)}, u32[]{:S(2)}, u32[]{:S(2)}) async-start(bf16[8,96,768]{2,1,0:T(8,128)(2,1)} %broadcast_in_dim.9), calls=%async_computation | async-start | bytes 2359296 | tf_op jit(solution)/shard_map/all_to_all | solution.py:35
  143.2 281.6 %all-gather.4.cloned.1.call-start = ((), (), s32[]{:S(2)}) async-start(), calls=%async_computation.3 | async-start | bytes 1769472 | tf_op jit(solution)/shard_map/all_gather | solution.py:77
  186.5 1.5 copy-start.1
  327.1 84.0 %copy-start = (f32[768,768]{1,0:T(8,128)S(1)}, f32[768,768]{1,0:T(8,128)}, u32[]{:S(2)}) copy-start(f32[768,768]{1,0:T(8,128)} %fusion.25) | copy-start | bytes 7077892
  413.2 7.9 %slice-start = ((s8[4718592]{0:T(1024)(128)(4,1)}), s8[4194304]{0:T(1024)(128)(4,1)S(1)}, s32[]{:S(2)}) async-start(s8[4718592]{0:T(1024)(128)(4,1)} %bitcast.89), calls=%async_computation.5 | async-start | bytes 8388608
  415.7 5.4 %slice-start.1 = ((s8[4718592]{0:T(1024)(128)(4,1)}), s8[524288]{0:T(1024)(128)(4,1)S(1)}, s32[]{:S(2)}) async-start(s8[4718592]{0:T(1024)(128)(4,1)} %bitcast.89), calls=%async_computation.6 | async-start | bytes 1048576
Sparse Core Ops, SparseCore 0:
  67.9 65.7 all-gather.5
Sparse Core Ops, SparseCore 1:
  145.5 45.1 all-gather.3
